TPU v7x, 16 devices: a 4x2x1 block of a 4x4x8 slice. The times are simulated.
16 devices in a mesh: batch: 2 (over y, z), time: 8 (over x, core).
Axes of the slice: x: 4, y: 2, z: 1, core: 2. Of those that a mesh axis runs over, the one named last changes fastest.
The devices are a block of a 4x4x8 slice.
Arguments:
- latent: bfloat16 [768, 4, 48, 128], P(('batch', 'time')), parts along dimension 0
- conv_w: bfloat16 [4, 3, 3, 3, 128, 128], replicated
- conv_b: float32 [4, 128], replicated
- norm_g: float32 [5, 128], replicated
- norm_b: float32 [5, 128], replicated
- attn_w: bfloat16 [4, 128, 128], replicated
- attn_b: float32 [4, 128], replicated
Outputs:
- output: bfloat16 [768, 4, 48, 128], P(('batch', 'time')), parts along dimension 0
There are 2 independent parts. A program takes and returns all parts, laid end to end along the dimension named above; an argument that names none is the same for every part.
All inputs are finite; a program needn't handle non-finite values.
Results may differ from a plain program's by a relative error of at most 0.0139455.
Values are sent between devices in bfloat16 or wider.
A program may use at most 768 MiB of HBM per device.

v0:
```python
import functools

import jax
import jax.numpy as jnp
from jax import lax
from jax.experimental import pallas as pl
from jax.experimental.pallas import tpu as pltpu
from jax.sharding import PartitionSpec as P

GROUPS = 32
NORM_EPS = 1e-6
TILE = 8
ATT = 24
CHUNKS = 4
HALO = 2
VMEM_LIMIT = 34 * 2**20
MESH_ID = pl.DeviceIdType.MESH
F32, BF16 = jnp.float32, jnp.bfloat16


def dot(a, b):
    return jnp.dot(a, b, preferred_element_type=F32)


def vreg_sum(value):
    return jnp.sum(value.reshape(-1, 8, value.shape[-1]), axis=0)


def add_sums(sums, value):
    return sums[0] + vreg_sum(value), sums[1] + vreg_sum(value * value)


def clear_act(acts, height, width):
    for act in acts:
        for f in range(act.shape[0]):
            for i in range(height + 1):
                act[f, i * (width + 8):i * (width + 8) + 8] = jnp.zeros((8, act.shape[2]), F32)


def norm_tile(src, dst, act, tile, coef):
    height, width, chan = src.shape[1:]
    block = width + 8
    mean, scale, shift = coef
    scale, shift = 0.5 * scale, 0.5 * shift
    for f in range(TILE + HALO):
        half = (src[tile * TILE + f].astype(F32) - mean) * scale + shift
        value = half + half * jnp.tanh(half)
        dst[:, f, :, chan:2 * chan] = value.astype(BF16)
        for i in range(height):
            act[f, i * block + 8:(i + 1) * block] = value[i]
        for i in range(height):
            for e in (0, 2):
                moved = act[f, i * block + 7 + e:i * block + 7 + e + width]
                dst[i, f, :, e * chan:(e + 1) * chan] = moved.astype(BF16)


def conv_tile(u, w, bias):
    height, _, width, chan = u.shape
    chan //= 3
    zero_w = jnp.zeros((chan, chan), BF16)

    def cols(row, first, count, e):
        return u[row, first:first + count, :, e * chan:(e + 1) * chan].reshape(count * width, chan)

    lhs, rhs = [], []
    for a in range(3):
        for e in range(3):
            for side in range(2):
                lhs.append(jnp.concatenate([cols(g + side, a, TILE, e) for g in range(0, height, 2)], axis=0))
                rhs.append(jnp.concatenate([w[a, 1 + side, e], w[a, side, e]], axis=1))
    main = dot(jnp.concatenate(lhs, axis=1), jnp.concatenate(rhs, axis=0))

    def extra(row, d):
        lhs, rhs = [], []
        for s in range(4):
            for e in range(3):
                lhs.append(jnp.concatenate([cols(row, 2 * p + s, 1, e) for p in range(TILE // 2)], axis=0))
                rhs.append(jnp.concatenate([w[s, d, e] if s < 3 else zero_w, w[s - 1, d, e] if s > 0 else zero_w], axis=1))
        return dot(jnp.concatenate(lhs, axis=1), jnp.concatenate(rhs, axis=0))

    lower = extra(2, 2)
    upper = extra(1, 0)
    rows = []
    for f in range(TILE):
        here = slice(f * width, (f + 1) * width)
        there = slice((TILE + f) * width, (TILE + f + 1) * width)
        pair = slice((f // 2) * width, (f // 2 + 1) * width)
        half = slice((f % 2) * chan, (f % 2 + 1) * chan)
        rows.append([main[here, :chan] + bias, main[here, chan:] + lower[pair, half] + bias, main[there, :chan] + upper[pair, half] + bias, main[there, chan:] + bias])
    return rows


def conv_stage(src, w, bias, coef, bufs, carry, emit, after):
    ua, ub, act_a, act_b = bufs
    tiles = (src.shape[0] - HALO) // TILE
    norm_tile(src, ua, act_a, tiles - 1, coef)

    def finish(u, tile, carry):
        rows = conv_tile(u, w, bias)
        for f in range(TILE):
            for i in range(len(rows[f])):
                carry = emit(tile * TILE + f, i, rows[f][i].astype(BF16), carry)
        return carry

    def body(it, carry):
        high = tiles - 1 - 2 * it
        norm_tile(src, ub, act_b, high - 1, coef)
        carry = finish(ua, high, carry)
        norm_tile(src, ua, act_a, jnp.maximum(high - 2, 0), coef)
        carry = finish(ub, high - 1, carry)
        after(it)
        return carry

    return lax.fori_loop(0, tiles // 2, body, carry)


def kernel(n_dev, latent, conv_w, conv_b, norm_g, norm_b, attn_w, attn_b, x_ref, h_ref, w_last, aux, ua, ub, act_a, act_b, qkv, probs, w_ref, aw_ref, cb_ref, g_ref, b_ref, ab_ref, halo, stats, in_sem, par_sem, halo_send, halo_recv, stat_send, stat_recv):
    frames, height, width, chan = latent.shape
    convs = conv_w.shape[0]
    tokens = height * width
    me = lax.axis_index("time")
    piece = frames // CHUNKS
    elem_count = n_dev * frames * tokens * (chan // GROUPS)
    bufs = (ua, ub, act_a, act_b)

    in_copies = [pltpu.make_async_copy(latent.at[pl.ds(c * piece, piece)], x_ref.at[pl.ds(HALO + c * piece, piece)], in_sem.at[c]) for c in range(CHUNKS)]
    for c in reversed(range(CHUNKS)):
        in_copies[c].start()
    barrier = pltpu.get_barrier_semaphore()
    for k in range(1, n_dev):
        pl.semaphore_signal(barrier, inc=1, device_id={"time": lax.rem(me + k, n_dev)}, device_id_type=MESH_ID)
    pairs = [(norm_g, g_ref), (norm_b, b_ref), (conv_b, cb_ref), (attn_w, aw_ref), (attn_b, ab_ref), (conv_w.at[pl.ds(0, convs - 1)], w_ref), (conv_w.at[convs - 1], w_last)]
    par_copies = [pltpu.make_async_copy(src, dst, par_sem.at[i]) for i, (src, dst) in enumerate(pairs)]
    for copy in par_copies:
        copy.start()
    clear_act((act_a, act_b), height, width)

    def halo_copy(slot, src):
        return pltpu.make_async_remote_copy(src_ref=src.at[pl.ds(frames, HALO)], dst_ref=halo.at[slot], send_sem=halo_send.at[slot], recv_sem=halo_recv.at[slot], device_id={"time": lax.rem(me + 1, n_dev)}, device_id_type=MESH_ID)

    def send_halo(slot, src):
        @pl.when(me < n_dev - 1)
        def _():
            halo_copy(slot, src).start()

    def take_halo(slot, src):
        @pl.when(me > 0)
        def _():
            halo_copy(slot, src).wait_recv()
            src[pl.ds(0, HALO)] = halo[slot]

        @pl.when(me == 0)
        def _():
            for f in range(HALO):
                src[f] = src[HALO]

        @pl.when(me < n_dev - 1)
        def _():
            halo_copy(slot, src).wait_send()

    lane = lax.broadcasted_iota(jnp.int32, (2, chan), 1)

    def exchange(stage, sums):
        stats[stage, me] = jnp.concatenate([jnp.sum(part, axis=0, keepdims=True) for part in sums], axis=0)

        def copy_to(k):
            return pltpu.make_async_remote_copy(src_ref=stats.at[stage, me], dst_ref=stats.at[stage, me], send_sem=stat_send.at[stage, k], recv_sem=stat_recv.at[stage, n_dev - k], device_id={"time": lax.rem(me + k, n_dev)}, device_id_type=MESH_ID)

        def copy_from(k):
            peer = lax.rem(me + k, n_dev)
            return pltpu.make_async_remote_copy(src_ref=stats.at[stage, peer], dst_ref=stats.at[stage, peer], send_sem=stat_send.at[stage, k], recv_sem=stat_recv.at[stage, k], device_id={"time": peer}, device_id_type=MESH_ID)

        for k in range(1, n_dev):
            copy_to(k).start()
        for k in range(1, n_dev):
            copy_from(k).wait_recv()
        total = stats[stage, 0]
        for d in range(1, n_dev):
            total = total + stats[stage, d]
        for k in range(1, n_dev):
            copy_to(k).wait_send()
        per_group = chan // GROUPS
        step = 1
        while step < per_group:
            swap = jnp.where(lax.rem(lane, 2 * step) < step, pltpu.roll(total, chan - step, 1), pltpu.roll(total, step, 1))
            total = total + swap
            step *= 2
        mean = total[0:1] / elem_count
        inv_std = lax.rsqrt(total[1:2] / elem_count - mean * mean + NORM_EPS)
        return mean, inv_std * g_ref[pl.ds(stage, 1)], b_ref[pl.ds(stage, 1)]

    def into(ref):
        def emit(frame, i, value, sums):
            ref[HALO + frame, i] = value
            return add_sums(sums, value.astype(F32))
        return emit

    def into_x(frame, i, value, sums):
        value = (x_ref[HALO + frame, i].astype(F32) + value.astype(F32)).astype(BF16)
        x_ref[HALO + frame, i] = value
        return add_sums(sums, value.astype(F32))

    def send_first(slot, src):
        def after(it):
            @pl.when(it == 0)
            def _():
                send_halo(slot, src)
        return after

    zero = jnp.zeros((8, chan), F32)
    sums = (zero, zero)
    for c in reversed(range(CHUNKS)):
        in_copies[c].wait()

        def add_frame(f, sums):
            return add_sums(sums, x_ref[HALO + c * piece + f].astype(F32))

        sums = lax.fori_loop(0, piece, add_frame, sums)
    with jax.named_scope("barrier"):
        pl.semaphore_wait(barrier, n_dev - 1)
    send_halo(0, x_ref)
    with jax.named_scope("par_wait"):
        for copy in par_copies:
            copy.wait()

    def conv(k, src, emit, after, coef):
        with jax.named_scope("conv"):
            return conv_stage(src, w_ref.at[k], cb_ref[pl.ds(k, 1)], coef, bufs, (zero, zero), emit, after)

    def renorm(stage, sums):
        with jax.named_scope("exchange"):
            return exchange(stage, sums)

    coef = renorm(0, sums)
    take_halo(0, x_ref)
    sums = conv(0, x_ref, into(h_ref), send_first(1, h_ref), coef)
    coef = renorm(1, sums)
    take_halo(1, h_ref)
    sums = conv(1, h_ref, into_x, lambda it: None, coef)
    mean, scale, shift = renorm(2, sums)

    qkv_w = jnp.concatenate([aw_ref[0], aw_ref[1], aw_ref[2]], axis=1)
    qkv_bias = jnp.concatenate([ab_ref[0:1], ab_ref[1:2], ab_ref[2:3]], axis=1)
    out_bias = ab_ref[3:4]
    gain = chan ** -0.5 * 1.4426950408889634
    pairs = ATT // 2

    def attend(it, sums):
        first = HALO + frames - ATT * (it + 1)
        scores, mixed = {}, {}

        def project(p):
            feature = x_ref[pl.ds(first + 2 * p, 2)].astype(F32).reshape(2 * tokens, chan)
            normed = ((feature - mean) * scale + shift).astype(BF16)
            qkv[p % 3] = (dot(normed, qkv_w) + qkv_bias).astype(BF16)

        def score(p):
            for f in range(2):
                mine = slice(f * tokens, (f + 1) * tokens)
                scores[p, f] = lax.dot_general(qkv[p % 3, mine, :chan], qkv[p % 3, mine, chan:2 * chan], (((1,), (1,)), ((), ())), preferred_element_type=F32)

        def softmax(p):
            for f in range(2):
                value = scores.pop((p, f))
                power = jnp.exp2((value - jnp.max(value, axis=1, keepdims=True)) * gain)
                probs[p % 2, f] = (power / jnp.sum(power, axis=1, keepdims=True)).astype(BF16)

        def mix(p):
            for f in range(2):
                mixed[p, f] = dot(probs[p % 2, f], qkv[p % 3, f * tokens:(f + 1) * tokens, 2 * chan:]).astype(BF16)

        def close(p, sums):
            branch = (dot(jnp.concatenate([mixed.pop((p, f)) for f in range(2)], axis=0), aw_ref[3]) + out_bias).astype(BF16)
            value = (x_ref[pl.ds(first + 2 * p, 2)].astype(F32).reshape(2 * tokens, chan) + branch.astype(F32)).astype(BF16)
            h_ref[pl.ds(first + 2 * p, 2)] = value.reshape(2, height, width, chan)
            return add_sums(sums, value.astype(F32))

        for step in range(pairs + 3):
            if 0 <= step - 1 < pairs:
                score(step - 1)
            if step < pairs:
                project(step)
            if 0 <= step - 2 < pairs:
                mix(step - 2)
            if 0 <= step - 1 < pairs:
                softmax(step - 1)
            if 0 <= step - 3 < pairs:
                sums = close(step - 3, sums)

        @pl.when(it == 0)
        def _():
            send_halo(2, h_ref)

        return sums

    with jax.named_scope("attention"):
        sums = lax.fori_loop(0, frames // ATT, attend, (zero, zero))
    coef = renorm(3, sums)
    take_halo(2, h_ref)
    sums = conv(2, h_ref, into(x_ref), send_first(3, x_ref), coef)
    coef = renorm(4, sums)
    take_halo(3, x_ref)
    aux[0:4] = jnp.concatenate([*coef, cb_ref[convs - 1:convs]], axis=0)


def last_kernel(h_ref, x_ref, w_ref, aux, out, y_ref, ua, ub, act_a, act_b, out_sem):
    frames, height, width, chan = y_ref.shape
    clear_act((act_a, act_b), height, width)
    coef = (aux[0:1], aux[1:2], aux[2:3])

    def out_copy(it):
        first = frames - 2 * TILE * (it + 1)
        return pltpu.make_async_copy(y_ref.at[pl.ds(first, 2 * TILE)], out.at[pl.ds(first, 2 * TILE)], out_sem.at[it])

    def into_y(frame, i, value, carry):
        y_ref[frame, i] = (x_ref[HALO + frame, i].astype(F32) + value.astype(F32)).astype(BF16)
        return carry

    with jax.named_scope("conv_last"):
        conv_stage(h_ref, w_ref, aux[3:4], coef, (ua, ub, act_a, act_b), 0, into_y, lambda it: out_copy(it).start())
    with jax.named_scope("drain"):
        for it in range(frames // TILE // 2):
            out_copy(it).wait()


def solution(mesh):
    n_dev = mesh.shape["time"]
    video_spec = P(("batch", "time"), None, None, None)

    def device_body(latent, conv_w, conv_b, norm_g, norm_b, attn_w, attn_b):
        frames, height, width, chan = latent.shape
        convs = conv_w.shape[0]
        hbm, vmem = pl.BlockSpec(memory_space=pltpu.HBM), pl.BlockSpec(memory_space=pltpu.VMEM)
        padded = (frames + HALO, height, width, chan)
        dma = pltpu.SemaphoreType.DMA
        bufs = [pltpu.VMEM((height, TILE + HALO, width, 3 * chan), BF16)] * 2 + [pltpu.VMEM((TILE + HALO, height * (width + 8) + 8, chan), F32)] * 2
        state = pl.pallas_call(
            functools.partial(kernel, n_dev),
            out_shape=[pltpu.VMEM(padded, BF16), pltpu.VMEM(padded, BF16), pltpu.VMEM(conv_w.shape[1:], BF16), pltpu.VMEM((8, chan), F32)],
            in_specs=[hbm] * 7,
            out_specs=[vmem] * 4,
            scratch_shapes=[
                *bufs,
                pltpu.VMEM((3, 2 * height * width, 3 * chan), BF16),
                pltpu.VMEM((2, 2, height * width, height * width), BF16),
                pltpu.VMEM((convs - 1, *conv_w.shape[1:]), BF16),
                pltpu.VMEM(attn_w.shape, BF16),
                pltpu.VMEM(conv_b.shape, F32),
                pltpu.VMEM(norm_g.shape, F32),
                pltpu.VMEM(norm_b.shape, F32),
                pltpu.VMEM(attn_b.shape, F32),
                pltpu.VMEM((4, HALO, height, width, chan), BF16),
                pltpu.VMEM((5, n_dev, 2, chan), F32),
                dma((CHUNKS,)),
                dma((7,)),
                dma((4,)),
                dma((4,)),
                dma((5, n_dev)),
                dma((5, n_dev)),
            ],
            compiler_params=pltpu.CompilerParams(collective_id=0, has_side_effects=True, vmem_limit_bytes=VMEM_LIMIT),
        )(latent, conv_w, conv_b, norm_g, norm_b, attn_w, attn_b)
        return pl.pallas_call(
            last_kernel,
            out_shape=jax.ShapeDtypeStruct(latent.shape, latent.dtype),
            in_specs=[vmem] * 4,
            out_specs=hbm,
            scratch_shapes=[pltpu.VMEM(latent.shape, BF16), *bufs, dma((frames // TILE // 2,))],
            compiler_params=pltpu.CompilerParams(vmem_limit_bytes=VMEM_LIMIT),
        )(*state)

    return jax.shard_map(device_body, mesh=mesh, in_specs=(video_spec, P(), P(), P(), P(), P(), P()), out_specs=video_spec, check_vma=False)
```

profile of v0, /device:TPU:113, one launch (start us, length us, event | category | flops | bytes accessed | tf_op | source)
XLA Modules:
  0.0 77.9 jit_solution(5870602223681999824)
XLA Ops:
  0.0 0.0 copy-start
  0.0 2.0 %copy-done = bf16[4,3,3,3,128,128]{5,4,3,2,1,0:T(8,128)(2,1)S(1)} copy-done((bf16[4,3,3,3,128,128]{5,4,3,2,1,0:T(8,128)(2,1)S(1)}, bf16[4,3,3,3,128,128]{5,4,3,2,1,0:T(8,128)(2,1)}, u32[]{:S(2)}) %copy-start) | copy-done | bytes 3538968
  2.0 0.0 copy-start.1
  2.0 1.7 %copy-done.1 = bf16[48,4,48,128]{3,2,1,0:T(8,128)(2,1)S(1)} copy-done((bf16[48,4,48,128]{3,2,1,0:T(8,128)(2,1)S(1)}, bf16[48,4,48,128]{3,2,1,0:T(8,128)(2,1)}, u32[]{:S(2)}) %copy-start.1) | copy-done | bytes 2359320
  3.7 0.0 copy-start.2
  3.7 0.9 %copy-done.2 = bf16[4,128,128]{2,1,0:T(8,128)(2,1)S(1)} copy-done((bf16[4,128,128]{2,1,0:T(8,128)(2,1)S(1)}, bf16[4,128,128]{2,1,0:T(8,128)(2,1)}, u32[]{:S(2)}) %copy-start.2) | copy-done | bytes 131096
  4.6 0.0 copy-start.3
  4.6 0.7 copy-done.3
  5.3 0.0 copy-start.4
  5.3 0.7 copy-done.4
  5.9 0.0 copy-start.5
  5.9 0.7 copy-done.5
  6.6 0.0 copy-start.6
  6.6 0.7 copy-done.6
  7.3 60.5 %shard_map.73 = (bf16[50,4,48,128]{3,2,1,0:T(8,128)(2,1)S(1)}, bf16[50,4,48,128]{3,2,1,0:T(8,128)(2,1)S(1)}, bf16[3,3,3,128,128]{4,3,2,1,0:T(8,128)(2,1)S(1)}, f32[8,128]{1,0:T(8,128)S(1)}) custom-call(bf16[48,4,48,128]{3,2,1,0:T(8,128)(2,1)S(1)} %copy-done.1, bf16[4,3,3,3,128,128]{5,4,3,2,1,0:T(8,128)(2,1)S(1)} %copy-done, f32[4,128]{1,0:T(4,128)S(1)} %copy-done.5, ...), custom_call_target="tpu_custom_call" | custom-call | tf_op jit(solution)/shard_map/pallas_call | solution.py:337
  67.8 9.9 %shard_map.74 = bf16[48,4,48,128]{3,2,1,0:T(8,128)(2,1)} custom-call(bf16[50,4,48,128]{3,2,1,0:T(8,128)(2,1)S(1)} %get-tuple-element.9.h_ref, bf16[50,4,48,128]{3,2,1,0:T(8,128)(2,1)S(1)} %get-tuple-element.10.x_ref, bf16[3,3,3,128,128]{4,3,2,1,0:T(8,128)(2,1)S(1)} %get-tuple-element.11.w_ref, f32[8,128]{1,0:T(8,128)S(1)} %get-tuple-element.12.aux), custom_call_target="tpu_custom_call" | custom-call | tf_op jit(solution)/shard_map/pallas_call | solution.py:363
Async XLA Ops:
  0.0 2.0 %copy-start = (bf16[4,3,3,3,128,128]{5,4,3,2,1,0:T(8,128)(2,1)S(1)}, bf16[4,3,3,3,128,128]{5,4,3,2,1,0:T(8,128)(2,1)}, u32[]{:S(2)}) copy-start(bf16[4,3,3,3,128,128]{5,4,3,2,1,0:T(8,128)(2,1)} %conv_w.1) | copy-start | bytes 10616836
  2.0 1.7 %copy-start.1 = (bf16[48,4,48,128]{3,2,1,0:T(8,128)(2,1)S(1)}, bf16[48,4,48,128]{3,2,1,0:T(8,128)(2,1)}, u32[]{:S(2)}) copy-start(bf16[48,4,48,128]{3,2,1,0:T(8,128)(2,1)} %latent.1) | copy-start | bytes 7077892
  3.7 0.9 %copy-start.2 = (bf16[4,128,128]{2,1,0:T(8,128)(2,1)S(1)}, bf16[4,128,128]{2,1,0:T(8,128)(2,1)}, u32[]{:S(2)}) copy-start(bf16[4,128,128]{2,1,0:T(8,128)(2,1)} %attn_w.1) | copy-start | bytes 393220
  4.6 0.7 copy-start.3
  5.3 0.7 copy-start.4
  5.9 0.7 copy-start.5
  6.6 0.7 copy-start.6
where the time goes:
time: 78.1 us; the launch traced here: 77.9 us
  Pallas kernels  70.4 us (90%)
  local copies, waits for them, and re-layouts  7.3 us (9%)
    pallas_call x1, Pallas kernels, device_body(): pl.pallas_call(functools.partial(kernel, n_dev), out_shape=[pltpu.VMEM(pa...  60.5 us
    pallas_call x1, Pallas kernels, device_body(): pl.pallas_call(last_kernel, out_shape=jax.ShapeDtypeStruct(latent.shape,...  9.92 us
    unnamed x14, local copies, waits for them, and re-layouts  7.3 us

commit v1 on v0

--- a/solution.py
+++ b/solution.py
@@ -359,7 +359,7 @@
                 dma((5, n_dev)),
             ],
             compiler_params=pltpu.CompilerParams(collective_id=0, has_side_effects=True, vmem_limit_bytes=VMEM_LIMIT),
-        )(latent, conv_w, conv_b, norm_g, norm_b, attn_w, attn_b)
+        )(*(pltpu.with_memory_space_constraint(value, pltpu.HBM) for value in (latent, conv_w, conv_b, norm_g, norm_b, attn_w, attn_b)))
         return pl.pallas_call(
             last_kernel,
             out_shape=jax.ShapeDtypeStruct(latent.shape, latent.dtype),

time: 78.1 us -> 70.4 us (0.901)
  local copies, waits for them, and re-layouts: 7.3 us -> 0 us
    unnamed x14 -> x0, local copies, waits for them, and re-layouts: 7.3 us -> none
where the time goes in v1:
time: 70.4 us; the launch traced here: 70.3 us
  Pallas kernels  70.2 us (100%)
    pallas_call x1, Pallas kernels, device_body(): pl.pallas_call(functools.partial(kernel, n_dev), out_shape=[pltpu.VMEM(pa...  60.2 us
    pallas_call x1, Pallas kernels, device_body(): pl.pallas_call(last_kernel, out_shape=jax.ShapeDtypeStruct(latent.shape,...  9.92 us

profile of v1, /device:TPU:113, one launch (start us, length us, event | category | flops | bytes accessed | tf_op | source)
XLA Modules:
  0.0 70.3 jit_solution(12141648311056953585)
XLA Ops:
  0.0 60.2 %shard_map.73 = (bf16[50,4,48,128]{3,2,1,0:T(8,128)(2,1)S(1)}, bf16[50,4,48,128]{3,2,1,0:T(8,128)(2,1)S(1)}, bf16[3,3,3,128,128]{4,3,2,1,0:T(8,128)(2,1)S(1)}, f32[8,128]{1,0:T(8,128)S(1)}) custom-call(bf16[48,4,48,128]{3,2,1,0:T(8,128)(2,1)} %latent.1, bf16[4,3,3,3,128,128]{5,4,3,2,1,0:T(8,128)(2,1)} %conv_w.1, f32[4,128]{1,0:T(4,128)} %conv_b.1, ...), custom_call_target="tpu_custom_call" | custom-call | tf_op jit(solution)/shard_map/pallas_call | solution.py:337
  60.3 9.9 %shard_map.74 = bf16[48,4,48,128]{3,2,1,0:T(8,128)(2,1)} custom-call(bf16[50,4,48,128]{3,2,1,0:T(8,128)(2,1)S(1)} %get-tuple-element.9.h_ref, bf16[50,4,48,128]{3,2,1,0:T(8,128)(2,1)S(1)} %get-tuple-element.10.x_ref, bf16[3,3,3,128,128]{4,3,2,1,0:T(8,128)(2,1)S(1)} %get-tuple-element.11.w_ref, f32[8,128]{1,0:T(8,128)S(1)} %get-tuple-element.12.aux), custom_call_target="tpu_custom_call" | custom-call | tf_op jit(solution)/shard_map/pallas_call | solution.py:363

commit v2 on v1

--- a/solution.py
+++ b/solution.py
@@ -11,7 +11,7 @@
 NORM_EPS = 1e-6
 TILE = 8
 ATT = 24
-CHUNKS = 4
+CHUNKS = 8
 HALO = 2
 VMEM_LIMIT = 34 * 2**20
 MESH_ID = pl.DeviceIdType.MESH
@@ -90,7 +90,7 @@
     return rows
 
 
-def conv_stage(src, w, bias, coef, bufs, carry, emit, after):
+def conv_stage(src, w, bias, coef, bufs, carry, emit, after, done=lambda tile: None):
     ua, ub, act_a, act_b = bufs
     tiles = (src.shape[0] - HALO) // TILE
     norm_tile(src, ua, act_a, tiles - 1, coef)
@@ -106,8 +106,10 @@
         high = tiles - 1 - 2 * it
         norm_tile(src, ub, act_b, high - 1, coef)
         carry = finish(ua, high, carry)
+        done(high)
         norm_tile(src, ua, act_a, jnp.maximum(high - 2, 0), coef)
         carry = finish(ub, high - 1, carry)
+        done(high - 1)
         after(it)
         return carry
 
@@ -131,7 +133,7 @@
         pl.semaphore_signal(barrier, inc=1, device_id={"time": lax.rem(me + k, n_dev)}, device_id_type=MESH_ID)
     pairs = [(norm_g, g_ref), (norm_b, b_ref), (conv_b, cb_ref), (attn_w, aw_ref), (attn_b, ab_ref), (conv_w.at[pl.ds(0, convs - 1)], w_ref), (conv_w.at[convs - 1], w_last)]
     par_copies = [pltpu.make_async_copy(src, dst, par_sem.at[i]) for i, (src, dst) in enumerate(pairs)]
-    for copy in par_copies:
+    for copy in par_copies[:-2]:
         copy.start()
     clear_act((act_a, act_b), height, width)
 
@@ -170,7 +172,7 @@
             peer = lax.rem(me + k, n_dev)
             return pltpu.make_async_remote_copy(src_ref=stats.at[stage, peer], dst_ref=stats.at[stage, peer], send_sem=stat_send.at[stage, k], recv_sem=stat_recv.at[stage, k], device_id={"time": peer}, device_id_type=MESH_ID)
 
-        for k in range(1, n_dev):
+        for k in sorted(range(1, n_dev), key=lambda k: abs(2 * k - n_dev)):
             copy_to(k).start()
         for k in range(1, n_dev):
             copy_from(k).wait_recv()
@@ -211,6 +213,9 @@
     sums = (zero, zero)
     for c in reversed(range(CHUNKS)):
         in_copies[c].wait()
+        if c == 0:
+            for copy in par_copies[-2:]:
+                copy.start()
 
         def add_frame(f, sums):
             return add_sums(sums, x_ref[HALO + c * piece + f].astype(F32))
@@ -252,12 +257,12 @@
         def project(p):
             feature = x_ref[pl.ds(first + 2 * p, 2)].astype(F32).reshape(2 * tokens, chan)
             normed = ((feature - mean) * scale + shift).astype(BF16)
-            qkv[p % 3] = (dot(normed, qkv_w) + qkv_bias).astype(BF16)
+            qkv[p % 4] = (dot(normed, qkv_w) + qkv_bias).astype(BF16)
 
         def score(p):
             for f in range(2):
                 mine = slice(f * tokens, (f + 1) * tokens)
-                scores[p, f] = lax.dot_general(qkv[p % 3, mine, :chan], qkv[p % 3, mine, chan:2 * chan], (((1,), (1,)), ((), ())), preferred_element_type=F32)
+                scores[p, f] = lax.dot_general(qkv[p % 4, mine, :chan], qkv[p % 4, mine, chan:2 * chan], (((1,), (1,)), ((), ())), preferred_element_type=F32)
 
         def softmax(p):
             for f in range(2):
@@ -267,7 +272,7 @@
 
         def mix(p):
             for f in range(2):
-                mixed[p, f] = dot(probs[p % 2, f], qkv[p % 3, f * tokens:(f + 1) * tokens, 2 * chan:]).astype(BF16)
+                mixed[p, f] = dot(probs[p % 2, f], qkv[p % 4, f * tokens:(f + 1) * tokens, 2 * chan:]).astype(BF16)
 
         def close(p, sums):
             branch = (dot(jnp.concatenate([mixed.pop((p, f)) for f in range(2)], axis=0), aw_ref[3]) + out_bias).astype(BF16)
@@ -275,17 +280,17 @@
             h_ref[pl.ds(first + 2 * p, 2)] = value.reshape(2, height, width, chan)
             return add_sums(sums, value.astype(F32))
 
-        for step in range(pairs + 3):
+        for step in range(pairs + 4):
             if 0 <= step - 1 < pairs:
                 score(step - 1)
-            if step < pairs:
-                project(step)
+            if 0 <= step - 0 < pairs:
+                project(step - 0)
+            if 0 <= step - 3 < pairs:
+                mix(step - 3)
             if 0 <= step - 2 < pairs:
-                mix(step - 2)
-            if 0 <= step - 1 < pairs:
-                softmax(step - 1)
-            if 0 <= step - 3 < pairs:
-                sums = close(step - 3, sums)
+                softmax(step - 2)
+            if 0 <= step - 4 < pairs:
+                sums = close(step - 4, sums)
 
         @pl.when(it == 0)
         def _():
@@ -308,19 +313,19 @@
     clear_act((act_a, act_b), height, width)
     coef = (aux[0:1], aux[1:2], aux[2:3])
 
-    def out_copy(it):
-        first = frames - 2 * TILE * (it + 1)
-        return pltpu.make_async_copy(y_ref.at[pl.ds(first, 2 * TILE)], out.at[pl.ds(first, 2 * TILE)], out_sem.at[it])
+    def out_copy(tile):
+        span = pl.ds(tile * TILE, TILE)
+        return pltpu.make_async_copy(y_ref.at[span], out.at[span], out_sem.at[tile])
 
     def into_y(frame, i, value, carry):
         y_ref[frame, i] = (x_ref[HALO + frame, i].astype(F32) + value.astype(F32)).astype(BF16)
         return carry
 
     with jax.named_scope("conv_last"):
-        conv_stage(h_ref, w_ref, aux[3:4], coef, (ua, ub, act_a, act_b), 0, into_y, lambda it: out_copy(it).start())
+        conv_stage(h_ref, w_ref, aux[3:4], coef, (ua, ub, act_a, act_b), 0, into_y, lambda it: None, lambda tile: out_copy(tile).start())
     with jax.named_scope("drain"):
-        for it in range(frames // TILE // 2):
-            out_copy(it).wait()
+        for tile in range(frames // TILE):
+            out_copy(tile).wait()
 
 
 def solution(mesh):
@@ -341,7 +346,7 @@
             out_specs=[vmem] * 4,
             scratch_shapes=[
                 *bufs,
-                pltpu.VMEM((3, 2 * height * width, 3 * chan), BF16),
+                pltpu.VMEM((4, 2 * height * width, 3 * chan), BF16),
                 pltpu.VMEM((2, 2, height * width, height * width), BF16),
                 pltpu.VMEM((convs - 1, *conv_w.shape[1:]), BF16),
                 pltpu.VMEM(attn_w.shape, BF16),
@@ -365,7 +370,7 @@
             out_shape=jax.ShapeDtypeStruct(latent.shape, latent.dtype),
             in_specs=[vmem] * 4,
             out_specs=hbm,
-            scratch_shapes=[pltpu.VMEM(latent.shape, BF16), *bufs, dma((frames // TILE // 2,))],
+            scratch_shapes=[pltpu.VMEM(latent.shape, BF16), *bufs, dma((frames // TILE,))],
             compiler_params=pltpu.CompilerParams(vmem_limit_bytes=VMEM_LIMIT),
         )(*state)
 

time: 70.4 us -> 71 us (level)
  no operation moved by 1% of the time
where the time goes in v2:
time: 71 us; the launch traced here: 70.9 us
  Pallas kernels  70.7 us (100%)
    pallas_call x1, Pallas kernels, device_body(): pl.pallas_call(functools.partial(kernel, n_dev), out_shape=[pltpu.VMEM(pa...  60.9 us
    pallas_call x1, Pallas kernels, device_body(): pl.pallas_call(last_kernel, out_shape=jax.ShapeDtypeStruct(latent.shape,...  9.83 us

profile of v2, /device:TPU:113, one launch (start us, length us, event | category | flops | bytes accessed | tf_op | source)
XLA Modules:
  0.0 70.9 jit_solution(4998982403219919315)
XLA Ops:
  0.0 60.9 %shard_map.73 = (bf16[50,4,48,128]{3,2,1,0:T(8,128)(2,1)S(1)}, bf16[50,4,48,128]{3,2,1,0:T(8,128)(2,1)S(1)}, bf16[3,3,3,128,128]{4,3,2,1,0:T(8,128)(2,1)S(1)}, f32[8,128]{1,0:T(8,128)S(1)}) custom-call(bf16[48,4,48,128]{3,2,1,0:T(8,128)(2,1)} %latent.1, bf16[4,3,3,3,128,128]{5,4,3,2,1,0:T(8,128)(2,1)} %conv_w.1, f32[4,128]{1,0:T(4,128)} %conv_b.1, ...), custom_call_target="tpu_custom_call" | custom-call | tf_op jit(solution)/shard_map/pallas_call | solution.py:342
  60.9 9.8 %shard_map.74 = bf16[48,4,48,128]{3,2,1,0:T(8,128)(2,1)} custom-call(bf16[50,4,48,128]{3,2,1,0:T(8,128)(2,1)S(1)} %get-tuple-element.9.h_ref, bf16[50,4,48,128]{3,2,1,0:T(8,128)(2,1)S(1)} %get-tuple-element.10.x_ref, bf16[3,3,3,128,128]{4,3,2,1,0:T(8,128)(2,1)S(1)} %get-tuple-element.11.w_ref, f32[8,128]{1,0:T(8,128)S(1)} %get-tuple-element.12.aux), custom_call_target="tpu_custom_call" | custom-call | tf_op jit(solution)/shard_map/pallas_call | solution.py:368

commit v3 on v2

--- a/solution.py
+++ b/solution.py
@@ -12,6 +12,7 @@
 TILE = 8
 ATT = 24
 CHUNKS = 8
+OUT_PIECES = 4
 HALO = 2
 VMEM_LIMIT = 34 * 2**20
 MESH_ID = pl.DeviceIdType.MESH
@@ -30,28 +31,20 @@
     return sums[0] + vreg_sum(value), sums[1] + vreg_sum(value * value)
 
 
-def clear_act(acts, height, width):
-    for act in acts:
-        for f in range(act.shape[0]):
-            for i in range(height + 1):
-                act[f, i * (width + 8):i * (width + 8) + 8] = jnp.zeros((8, act.shape[2]), F32)
-
-
-def norm_tile(src, dst, act, tile, coef):
+def norm_tile(src, dst, tile, coef):
     height, width, chan = src.shape[1:]
-    block = width + 8
     mean, scale, shift = coef
     scale, shift = 0.5 * scale, 0.5 * shift
+    row = lax.broadcasted_iota(jnp.int32, (8, chan), 0)
     for f in range(TILE + HALO):
         half = (src[tile * TILE + f].astype(F32) - mean) * scale + shift
         value = half + half * jnp.tanh(half)
         dst[:, f, :, chan:2 * chan] = value.astype(BF16)
         for i in range(height):
-            act[f, i * block + 8:(i + 1) * block] = value[i]
-        for i in range(height):
-            for e in (0, 2):
-                moved = act[f, i * block + 7 + e:i * block + 7 + e + width]
-                dst[i, f, :, e * chan:(e + 1) * chan] = moved.astype(BF16)
+            gap = jnp.zeros((1, chan), F32)
+            left, right = jnp.concatenate([gap, value[i][:width - 1]], axis=0), jnp.concatenate([value[i][1:], gap], axis=0)
+            dst[i, f, :, :chan] = left.astype(BF16)
+            dst[i, f, :, 2 * chan:] = right.astype(BF16)
 
 
 def conv_tile(u, w, bias):
@@ -91,9 +84,9 @@
 
 
 def conv_stage(src, w, bias, coef, bufs, carry, emit, after, done=lambda tile: None):
-    ua, ub, act_a, act_b = bufs
+    ua, ub = bufs
     tiles = (src.shape[0] - HALO) // TILE
-    norm_tile(src, ua, act_a, tiles - 1, coef)
+    norm_tile(src, ua, tiles - 1, coef)
 
     def finish(u, tile, carry):
         rows = conv_tile(u, w, bias)
@@ -104,10 +97,10 @@
 
     def body(it, carry):
         high = tiles - 1 - 2 * it
-        norm_tile(src, ub, act_b, high - 1, coef)
+        norm_tile(src, ub, high - 1, coef)
         carry = finish(ua, high, carry)
         done(high)
-        norm_tile(src, ua, act_a, jnp.maximum(high - 2, 0), coef)
+        norm_tile(src, ua, jnp.maximum(high - 2, 0), coef)
         carry = finish(ub, high - 1, carry)
         done(high - 1)
         after(it)
@@ -116,14 +109,14 @@
     return lax.fori_loop(0, tiles // 2, body, carry)
 
 
-def kernel(n_dev, latent, conv_w, conv_b, norm_g, norm_b, attn_w, attn_b, x_ref, h_ref, w_last, aux, ua, ub, act_a, act_b, qkv, probs, w_ref, aw_ref, cb_ref, g_ref, b_ref, ab_ref, halo, stats, in_sem, par_sem, halo_send, halo_recv, stat_send, stat_recv):
+def kernel(n_dev, latent, conv_w, conv_b, norm_g, norm_b, attn_w, attn_b, x_ref, h_ref, w_last, aux, ua, ub, qkv, probs, w_ref, aw_ref, cb_ref, g_ref, b_ref, ab_ref, halo, stats, in_sem, par_sem, halo_send, halo_recv, stat_send, stat_recv):
     frames, height, width, chan = latent.shape
     convs = conv_w.shape[0]
     tokens = height * width
     me = lax.axis_index("time")
     piece = frames // CHUNKS
     elem_count = n_dev * frames * tokens * (chan // GROUPS)
-    bufs = (ua, ub, act_a, act_b)
+    bufs = (ua, ub)
 
     in_copies = [pltpu.make_async_copy(latent.at[pl.ds(c * piece, piece)], x_ref.at[pl.ds(HALO + c * piece, piece)], in_sem.at[c]) for c in range(CHUNKS)]
     for c in reversed(range(CHUNKS)):
@@ -135,7 +128,6 @@
     par_copies = [pltpu.make_async_copy(src, dst, par_sem.at[i]) for i, (src, dst) in enumerate(pairs)]
     for copy in par_copies[:-2]:
         copy.start()
-    clear_act((act_a, act_b), height, width)
 
     def halo_copy(slot, src):
         return pltpu.make_async_remote_copy(src_ref=src.at[pl.ds(frames, HALO)], dst_ref=halo.at[slot], send_sem=halo_send.at[slot], recv_sem=halo_recv.at[slot], device_id={"time": lax.rem(me + 1, n_dev)}, device_id_type=MESH_ID)
@@ -182,11 +174,9 @@
         for k in range(1, n_dev):
             copy_to(k).wait_send()
         per_group = chan // GROUPS
-        step = 1
-        while step < per_group:
-            swap = jnp.where(lax.rem(lane, 2 * step) < step, pltpu.roll(total, chan - step, 1), pltpu.roll(total, step, 1))
-            total = total + swap
-            step *= 2
+        place, own = lax.rem(lane, per_group), total
+        for d in range(1, per_group):
+            total = total + jnp.where(place >= d, pltpu.roll(own, d, 1), 0.0) + jnp.where(place < per_group - d, pltpu.roll(own, chan - d, 1), 0.0)
         mean = total[0:1] / elem_count
         inv_std = lax.rsqrt(total[1:2] / elem_count - mean * mean + NORM_EPS)
         return mean, inv_std * g_ref[pl.ds(stage, 1)], b_ref[pl.ds(stage, 1)]
@@ -217,16 +207,13 @@
             for copy in par_copies[-2:]:
                 copy.start()
 
-        def add_frame(f, sums):
-            return add_sums(sums, x_ref[HALO + c * piece + f].astype(F32))
-
-        sums = lax.fori_loop(0, piece, add_frame, sums)
+        for f in range(piece):
+            sums = add_sums(sums, x_ref[HALO + c * piece + f].astype(F32))
     with jax.named_scope("barrier"):
         pl.semaphore_wait(barrier, n_dev - 1)
     send_halo(0, x_ref)
-    with jax.named_scope("par_wait"):
-        for copy in par_copies:
-            copy.wait()
+    for copy in par_copies[:-2]:
+        copy.wait()
 
     def conv(k, src, emit, after, coef):
         with jax.named_scope("conv"):
@@ -238,6 +225,8 @@
 
     coef = renorm(0, sums)
     take_halo(0, x_ref)
+    for copy in par_copies[-2:]:
+        copy.wait()
     sums = conv(0, x_ref, into(h_ref), send_first(1, h_ref), coef)
     coef = renorm(1, sums)
     take_halo(1, h_ref)
@@ -281,14 +270,14 @@
             return add_sums(sums, value.astype(F32))
 
         for step in range(pairs + 4):
+            if 0 <= step - 0 < pairs:
+                project(step - 0)
             if 0 <= step - 1 < pairs:
                 score(step - 1)
-            if 0 <= step - 0 < pairs:
-                project(step - 0)
+            if 0 <= step - 2 < pairs:
+                softmax(step - 2)
             if 0 <= step - 3 < pairs:
                 mix(step - 3)
-            if 0 <= step - 2 < pairs:
-                softmax(step - 2)
             if 0 <= step - 4 < pairs:
                 sums = close(step - 4, sums)
 
@@ -308,24 +297,31 @@
     aux[0:4] = jnp.concatenate([*coef, cb_ref[convs - 1:convs]], axis=0)
 
 
-def last_kernel(h_ref, x_ref, w_ref, aux, out, y_ref, ua, ub, act_a, act_b, out_sem):
+def last_kernel(h_ref, x_ref, w_ref, aux, out, y_ref, ua, ub, out_sem):
     frames, height, width, chan = y_ref.shape
-    clear_act((act_a, act_b), height, width)
     coef = (aux[0:1], aux[1:2], aux[2:3])
 
-    def out_copy(tile):
-        span = pl.ds(tile * TILE, TILE)
-        return pltpu.make_async_copy(y_ref.at[span], out.at[span], out_sem.at[tile])
+    share = TILE // OUT_PIECES
+
+    def out_copies(tile):
+        for n in range(OUT_PIECES):
+            span = pl.ds(tile * TILE + n * share, share)
+            yield pltpu.make_async_copy(y_ref.at[span], out.at[span], out_sem.at[tile, n])
+
+    def write_out(tile):
+        for copy in out_copies(tile):
+            copy.start()
 
     def into_y(frame, i, value, carry):
         y_ref[frame, i] = (x_ref[HALO + frame, i].astype(F32) + value.astype(F32)).astype(BF16)
         return carry
 
     with jax.named_scope("conv_last"):
-        conv_stage(h_ref, w_ref, aux[3:4], coef, (ua, ub, act_a, act_b), 0, into_y, lambda it: None, lambda tile: out_copy(tile).start())
+        conv_stage(h_ref, w_ref, aux[3:4], coef, (ua, ub), 0, into_y, lambda it: None, write_out)
     with jax.named_scope("drain"):
         for tile in range(frames // TILE):
-            out_copy(tile).wait()
+            for copy in out_copies(tile):
+                copy.wait()
 
 
 def solution(mesh):
@@ -338,7 +334,7 @@
         hbm, vmem = pl.BlockSpec(memory_space=pltpu.HBM), pl.BlockSpec(memory_space=pltpu.VMEM)
         padded = (frames + HALO, height, width, chan)
         dma = pltpu.SemaphoreType.DMA
-        bufs = [pltpu.VMEM((height, TILE + HALO, width, 3 * chan), BF16)] * 2 + [pltpu.VMEM((TILE + HALO, height * (width + 8) + 8, chan), F32)] * 2
+        bufs = [pltpu.VMEM((height, TILE + HALO, width, 3 * chan), BF16)] * 2
         state = pl.pallas_call(
             functools.partial(kernel, n_dev),
             out_shape=[pltpu.VMEM(padded, BF16), pltpu.VMEM(padded, BF16), pltpu.VMEM(conv_w.shape[1:], BF16), pltpu.VMEM((8, chan), F32)],
@@ -370,7 +366,7 @@
             out_shape=jax.ShapeDtypeStruct(latent.shape, latent.dtype),
             in_specs=[vmem] * 4,
             out_specs=hbm,
-            scratch_shapes=[pltpu.VMEM(latent.shape, BF16), *bufs, dma((frames // TILE,))],
+            scratch_shapes=[pltpu.VMEM(latent.shape, BF16), *bufs, dma((frames // TILE, OUT_PIECES))],
             compiler_params=pltpu.CompilerParams(vmem_limit_bytes=VMEM_LIMIT),
         )(*state)
 

time: 71 us -> 66.2 us (0.932)
  Pallas kernels: 70.7 us -> 66 us
    pallas_call x1, Pallas kernels: 60.9 us -> 56.3 us  [device_body(): pl.pallas_call(functools.partial(kernel, n_dev), out_shape=[pltpu.VMEM(pa...]
where the time goes in v3:
time: 66.2 us; the launch traced here: 66.1 us
  Pallas kernels  66 us (100%)
    pallas_call x1, Pallas kernels, device_body(): pl.pallas_call(functools.partial(kernel, n_dev), out_shape=[pltpu.VMEM(pa...  56.3 us
    pallas_call x1, Pallas kernels, device_body(): pl.pallas_call(last_kernel, out_shape=jax.ShapeDtypeStruct(latent.shape,...  9.67 us

profile of v3, /device:TPU:113, one launch (start us, length us, event | category | flops | bytes accessed | tf_op | source)
XLA Modules:
  0.0 66.1 jit_solution(17237583582456454805)
XLA Ops:
  0.0 56.3 %shard_map.73 = (bf16[50,4,48,128]{3,2,1,0:T(8,128)(2,1)S(1)}, bf16[50,4,48,128]{3,2,1,0:T(8,128)(2,1)S(1)}, bf16[3,3,3,128,128]{4,3,2,1,0:T(8,128)(2,1)S(1)}, f32[8,128]{1,0:T(8,128)S(1)}) custom-call(bf16[48,4,48,128]{3,2,1,0:T(8,128)(2,1)} %latent.1, bf16[4,3,3,3,128,128]{5,4,3,2,1,0:T(8,128)(2,1)} %conv_w.1, f32[4,128]{1,0:T(4,128)} %conv_b.1, ...), custom_call_target="tpu_custom_call" | custom-call | tf_op jit(solution)/shard_map/pallas_call | solution.py:338
  56.3 9.7 %shard_map.74 = bf16[48,4,48,128]{3,2,1,0:T(8,128)(2,1)} custom-call(bf16[50,4,48,128]{3,2,1,0:T(8,128)(2,1)S(1)} %get-tuple-element.9.h_ref, bf16[50,4,48,128]{3,2,1,0:T(8,128)(2,1)S(1)} %get-tuple-element.10.x_ref, bf16[3,3,3,128,128]{4,3,2,1,0:T(8,128)(2,1)S(1)} %get-tuple-element.11.w_ref, f32[8,128]{1,0:T(8,128)S(1)} %get-tuple-element.12.aux), custom_call_target="tpu_custom_call" | custom-call | tf_op jit(solution)/shard_map/pallas_call | solution.py:364

commit v4 on v3

--- a/solution.py
+++ b/solution.py
@@ -35,16 +35,18 @@
     height, width, chan = src.shape[1:]
     mean, scale, shift = coef
     scale, shift = 0.5 * scale, 0.5 * shift
-    row = lax.broadcasted_iota(jnp.int32, (8, chan), 0)
+    width = src.shape[2]
+    first = lax.broadcasted_iota(jnp.int32, (8, chan), 0) == 0
+    final = lax.broadcasted_iota(jnp.int32, (8, chan), 0) == 7
     for f in range(TILE + HALO):
         half = (src[tile * TILE + f].astype(F32) - mean) * scale + shift
         value = half + half * jnp.tanh(half)
         dst[:, f, :, chan:2 * chan] = value.astype(BF16)
         for i in range(height):
-            gap = jnp.zeros((1, chan), F32)
-            left, right = jnp.concatenate([gap, value[i][:width - 1]], axis=0), jnp.concatenate([value[i][1:], gap], axis=0)
-            dst[i, f, :, :chan] = left.astype(BF16)
-            dst[i, f, :, 2 * chan:] = right.astype(BF16)
+            wrapped = jnp.where(first, 0.0, pltpu.roll(value[i, width - 8:], 1, 0))
+            dst[i, f, :, :chan] = jnp.concatenate([wrapped, value[i, :width - 8]], axis=0).astype(BF16)
+            wrapped = jnp.where(final, 0.0, pltpu.roll(value[i, :8], 7, 0))
+            dst[i, f, :, 2 * chan:] = jnp.concatenate([value[i, 8:], wrapped], axis=0).astype(BF16)
 
 
 def conv_tile(u, w, bias):
@@ -109,7 +111,7 @@
     return lax.fori_loop(0, tiles // 2, body, carry)
 
 
-def kernel(n_dev, latent, conv_w, conv_b, norm_g, norm_b, attn_w, attn_b, x_ref, h_ref, w_last, aux, ua, ub, qkv, probs, w_ref, aw_ref, cb_ref, g_ref, b_ref, ab_ref, halo, stats, in_sem, par_sem, halo_send, halo_recv, stat_send, stat_recv):
+def kernel(n_dev, latent, conv_w, conv_b, norm_g, norm_b, attn_w, attn_b, x_ref, h_ref, w_last, aux, raw, flat, ua, ub, qkv, probs, w_ref, aw_ref, cb_ref, g_ref, b_ref, ab_ref, halo, stats, in_sem, par_sem, halo_send, halo_recv, stat_send, stat_recv):
     frames, height, width, chan = latent.shape
     convs = conv_w.shape[0]
     tokens = height * width
@@ -118,7 +120,7 @@
     elem_count = n_dev * frames * tokens * (chan // GROUPS)
     bufs = (ua, ub)
 
-    in_copies = [pltpu.make_async_copy(latent.at[pl.ds(c * piece, piece)], x_ref.at[pl.ds(HALO + c * piece, piece)], in_sem.at[c]) for c in range(CHUNKS)]
+    in_copies = [pltpu.make_async_copy(latent.at[pl.ds(c * piece, piece)], raw.at[pl.ds(c * piece, piece)], in_sem.at[c]) for c in range(CHUNKS)]
     for c in reversed(range(CHUNKS)):
         in_copies[c].start()
     barrier = pltpu.get_barrier_semaphore()
@@ -208,7 +210,11 @@
                 copy.start()
 
         for f in range(piece):
-            sums = add_sums(sums, x_ref[HALO + c * piece + f].astype(F32))
+            value = raw[c * piece + f].astype(F32)
+            sums = add_sums(sums, value)
+            flat[f] = value
+            value = jnp.concatenate([flat[f, :, pl.ds(v, 8, stride=width // 8)] for v in range(width // 8)], axis=1)
+            x_ref[HALO + c * piece + f] = value.astype(BF16)
     with jax.named_scope("barrier"):
         pl.semaphore_wait(barrier, n_dev - 1)
     send_halo(0, x_ref)
@@ -297,7 +303,7 @@
     aux[0:4] = jnp.concatenate([*coef, cb_ref[convs - 1:convs]], axis=0)
 
 
-def last_kernel(h_ref, x_ref, w_ref, aux, out, y_ref, ua, ub, out_sem):
+def last_kernel(h_ref, x_ref, w_ref, aux, out, y_ref, flat, ua, ub, out_sem):
     frames, height, width, chan = y_ref.shape
     coef = (aux[0:1], aux[1:2], aux[2:3])
 
@@ -313,7 +319,11 @@
             copy.start()
 
     def into_y(frame, i, value, carry):
-        y_ref[frame, i] = (x_ref[HALO + frame, i].astype(F32) + value.astype(F32)).astype(BF16)
+        value = (x_ref[HALO + frame, i].astype(F32) + value.astype(F32)).astype(BF16).astype(F32)
+        slot = i % 2
+        for v in range(width // 8):
+            flat[slot, pl.ds(v, 8, stride=width // 8)] = value[8 * v:8 * v + 8]
+        y_ref[frame, i] = flat[slot].astype(BF16)
         return carry
 
     with jax.named_scope("conv_last"):
@@ -341,6 +351,8 @@
             in_specs=[hbm] * 7,
             out_specs=[vmem] * 4,
             scratch_shapes=[
+                pltpu.VMEM(latent.shape, BF16),
+                pltpu.VMEM((frames // CHUNKS, height, width, chan), F32),
                 *bufs,
                 pltpu.VMEM((4, 2 * height * width, 3 * chan), BF16),
                 pltpu.VMEM((2, 2, height * width, height * width), BF16),
@@ -366,7 +378,7 @@
             out_shape=jax.ShapeDtypeStruct(latent.shape, latent.dtype),
             in_specs=[vmem] * 4,
             out_specs=hbm,
-            scratch_shapes=[pltpu.VMEM(latent.shape, BF16), *bufs, dma((frames // TILE, OUT_PIECES))],
+            scratch_shapes=[pltpu.VMEM(latent.shape, BF16), pltpu.VMEM((2, width, chan), F32), *bufs, dma((frames // TILE, OUT_PIECES))],
             compiler_params=pltpu.CompilerParams(vmem_limit_bytes=VMEM_LIMIT),
         )(*state)
 

time: 66.2 us -> 65 us (0.982)
  Pallas kernels: 66 us -> 64.7 us
    pallas_call x1, Pallas kernels: 56.3 us -> 55.1 us  [device_body(): pl.pallas_call(functools.partial(kernel, n_dev), out_shape=[pltpu.VMEM(pa...]
where the time goes in v4:
time: 65 us; the launch traced here: 64.9 us
  Pallas kernels  64.7 us (100%)
    pallas_call x1, Pallas kernels, device_body(): pl.pallas_call(functools.partial(kernel, n_dev), out_shape=[pltpu.VMEM(pa...  55.1 us
    pallas_call x1, Pallas kernels, device_body(): pl.pallas_call(last_kernel, out_shape=jax.ShapeDtypeStruct(latent.shape,...  9.64 us

profile of v4, /device:TPU:113, one launch (start us, length us, event | category | flops | bytes accessed | tf_op | source)
XLA Modules:
  0.0 64.9 jit_solution(15583711827116647521)
XLA Ops:
  0.0 55.1 %shard_map.73 = (bf16[50,4,48,128]{3,2,1,0:T(8,128)(2,1)S(1)}, bf16[50,4,48,128]{3,2,1,0:T(8,128)(2,1)S(1)}, bf16[3,3,3,128,128]{4,3,2,1,0:T(8,128)(2,1)S(1)}, f32[8,128]{1,0:T(8,128)S(1)}) custom-call(bf16[48,4,48,128]{3,2,1,0:T(8,128)(2,1)} %latent.1, bf16[4,3,3,3,128,128]{5,4,3,2,1,0:T(8,128)(2,1)} %conv_w.1, f32[4,128]{1,0:T(4,128)} %conv_b.1, ...), custom_call_target="tpu_custom_call" | custom-call | tf_op jit(solution)/shard_map/pallas_call | solution.py:348
  55.1 9.6 %shard_map.74 = bf16[48,4,48,128]{3,2,1,0:T(8,128)(2,1)} custom-call(bf16[50,4,48,128]{3,2,1,0:T(8,128)(2,1)S(1)} %get-tuple-element.9.h_ref, bf16[50,4,48,128]{3,2,1,0:T(8,128)(2,1)S(1)} %get-tuple-element.10.x_ref, bf16[3,3,3,128,128]{4,3,2,1,0:T(8,128)(2,1)S(1)} %get-tuple-element.11.w_ref, f32[8,128]{1,0:T(8,128)S(1)} %get-tuple-element.12.aux), custom_call_target="tpu_custom_call" | custom-call | tf_op jit(solution)/shard_map/pallas_call | solution.py:376

commit v5 on v4

--- a/solution.py
+++ b/solution.py
@@ -156,7 +156,7 @@
 
     lane = lax.broadcasted_iota(jnp.int32, (2, chan), 1)
 
-    def exchange(stage, sums):
+    def exchange(stage, sums, meanwhile):
         stats[stage, me] = jnp.concatenate([jnp.sum(part, axis=0, keepdims=True) for part in sums], axis=0)
 
         def copy_to(k):
@@ -168,6 +168,7 @@
 
         for k in sorted(range(1, n_dev), key=lambda k: abs(2 * k - n_dev)):
             copy_to(k).start()
+        meanwhile()
         for k in range(1, n_dev):
             copy_from(k).wait_recv()
         total = stats[stage, 0]
@@ -210,32 +211,38 @@
                 copy.start()
 
         for f in range(piece):
-            value = raw[c * piece + f].astype(F32)
-            sums = add_sums(sums, value)
-            flat[f] = value
-            value = jnp.concatenate([flat[f, :, pl.ds(v, 8, stride=width // 8)] for v in range(width // 8)], axis=1)
-            x_ref[HALO + c * piece + f] = value.astype(BF16)
+            sums = add_sums(sums, raw[c * piece + f].astype(F32))
     with jax.named_scope("barrier"):
         pl.semaphore_wait(barrier, n_dev - 1)
-    send_halo(0, x_ref)
-    for copy in par_copies[:-2]:
-        copy.wait()
+
+    def reorder(n):
+        start = frames - piece * (n + 1)
+        for f in range(piece):
+            flat[f] = raw[start + f].astype(F32)
+            value = jnp.concatenate([flat[f, :, pl.ds(v, 8, stride=width // 8)] for v in range(width // 8)], axis=1)
+            x_ref[HALO + start + f] = value.astype(BF16)
+
+    def while_sums_travel():
+        reorder(0)
+        reorder(1)
+        send_halo(0, x_ref)
+        for n in range(2, CHUNKS):
+            reorder(n)
+        for copy in par_copies:
+            copy.wait()
+        take_halo(0, x_ref)
 
     def conv(k, src, emit, after, coef):
         with jax.named_scope("conv"):
             return conv_stage(src, w_ref.at[k], cb_ref[pl.ds(k, 1)], coef, bufs, (zero, zero), emit, after)
 
-    def renorm(stage, sums):
+    def renorm(stage, sums, meanwhile=lambda: None):
         with jax.named_scope("exchange"):
-            return exchange(stage, sums)
-
-    coef = renorm(0, sums)
-    take_halo(0, x_ref)
-    for copy in par_copies[-2:]:
-        copy.wait()
+            return exchange(stage, sums, meanwhile)
+
+    coef = renorm(0, sums, while_sums_travel)
     sums = conv(0, x_ref, into(h_ref), send_first(1, h_ref), coef)
-    coef = renorm(1, sums)
-    take_halo(1, h_ref)
+    coef = renorm(1, sums, lambda: take_halo(1, h_ref))
     sums = conv(1, h_ref, into_x, lambda it: None, coef)
     mean, scale, shift = renorm(2, sums)
 
@@ -295,11 +302,9 @@
 
     with jax.named_scope("attention"):
         sums = lax.fori_loop(0, frames // ATT, attend, (zero, zero))
-    coef = renorm(3, sums)
-    take_halo(2, h_ref)
+    coef = renorm(3, sums, lambda: take_halo(2, h_ref))
     sums = conv(2, h_ref, into(x_ref), send_first(3, x_ref), coef)
-    coef = renorm(4, sums)
-    take_halo(3, x_ref)
+    coef = renorm(4, sums, lambda: take_halo(3, x_ref))
     aux[0:4] = jnp.concatenate([*coef, cb_ref[convs - 1:convs]], axis=0)
 
 

time: 65 us -> 64.4 us (level)
  no operation moved by 1% of the time
where the time goes in v5:
time: 64.4 us; the launch traced here: 64.3 us
  Pallas kernels  64.1 us (100%)
    pallas_call x1, Pallas kernels, device_body(): pl.pallas_call(functools.partial(kernel, n_dev), out_shape=[pltpu.VMEM(pa...  54.4 us
    pallas_call x1, Pallas kernels, device_body(): pl.pallas_call(last_kernel, out_shape=jax.ShapeDtypeStruct(latent.shape,...  9.64 us

profile of v5, /device:TPU:113, one launch (start us, length us, event | category | flops | bytes accessed | tf_op | source)
XLA Modules:
  0.0 64.3 jit_solution(13823452731354698064)
XLA Ops:
  0.0 54.4 %shard_map.73 = (bf16[50,4,48,128]{3,2,1,0:T(8,128)(2,1)S(1)}, bf16[50,4,48,128]{3,2,1,0:T(8,128)(2,1)S(1)}, bf16[3,3,3,128,128]{4,3,2,1,0:T(8,128)(2,1)S(1)}, f32[8,128]{1,0:T(8,128)S(1)}) custom-call(bf16[48,4,48,128]{3,2,1,0:T(8,128)(2,1)} %latent.1, bf16[4,3,3,3,128,128]{5,4,3,2,1,0:T(8,128)(2,1)} %conv_w.1, f32[4,128]{1,0:T(4,128)} %conv_b.1, ...), custom_call_target="tpu_custom_call" | custom-call | tf_op jit(solution)/shard_map/pallas_call | solution.py:353
  54.5 9.6 %shard_map.74 = bf16[48,4,48,128]{3,2,1,0:T(8,128)(2,1)} custom-call(bf16[50,4,48,128]{3,2,1,0:T(8,128)(2,1)S(1)} %get-tuple-element.9.h_ref, bf16[50,4,48,128]{3,2,1,0:T(8,128)(2,1)S(1)} %get-tuple-element.10.x_ref, bf16[3,3,3,128,128]{4,3,2,1,0:T(8,128)(2,1)S(1)} %get-tuple-element.11.w_ref, f32[8,128]{1,0:T(8,128)S(1)} %get-tuple-element.12.aux), custom_call_target="tpu_custom_call" | custom-call | tf_op jit(solution)/shard_map/pallas_call | solution.py:381
